TPU v7x, 32 devices: a whole 2x2x4 slice. The times are simulated.
32 devices in a mesh: row: 4 (over z), col: 8 (over y, x, core).
Axes of the slice: x: 2, y: 2, z: 4, core: 2. Of those that a mesh axis runs over, the one named last changes fastest.
Arguments:
- neighbor: int32 [32, 3072, 3072], P(None, 'col', 'row'), may hold values from 0 to 1, as said below
- true_coords: float32 [32, 3, 3072], P(None, None, ('row', 'col')), as said below
- pred_coords: float32 [32, 3, 3072], P(None, None, ('row', 'col')), as said below
- residue_mask: int32 [32, 3072], P(None, ('row', 'col')), may hold values from 0 to 1, as said below
- single: bfloat16 [32, 3072, 384], P(None, ('row', 'col'))
- ln_gain: float32 [384], replicated, may hold values from 0.1 to 1.9
- w_hidden: bfloat16 [384, 128], replicated, may hold values from -0.3125 to 0.3125
- b_hidden: float32 [128], replicated, may hold values from -3 to 3
- w_mid: bfloat16 [128, 128], replicated, may hold values from -0.5 to 0.5
- b_mid: float32 [128], replicated, may hold values from -3 to 3
- w_logits: bfloat16 [128, 50], replicated, may hold values from -1.5 to 1.5
- b_logits: float32 [50], replicated, may hold values from -4 to 4
Outputs:
- lddt_score: float32 [32, 3072], P(None, ('row', 'col'))
- residue_loss: float32 [32, 3072], P(None, ('row', 'col'))
- total_loss: float32 [], replicated
Inputs may be any that keep to these rules, and one draw needn't show every extreme that they name: `neighbor`: 0 or 1; 0 where j == i; 1 wherever 0 < |i - j| <= 8. `residue_mask`: per structure, 1 on a leading run of 1536 or more residues and 0 after it. `true_coords`: positions in angstroms. `pred_coords`: positions in angstroms.
All inputs are finite; a program needn't handle non-finite values.
Results may differ from a plain program's by a relative error of at most 0.00098.
Values sent between devices are 32-bit elements; how exact they have to be, the bound alone decides.
A program may use at most 128 MiB of HBM per device.

v0:
```python
import jax
import jax.numpy as jnp
from jax import lax
from jax.sharding import PartitionSpec as P

L = 3072
THRESHOLDS = (0.5, 1.0, 2.0, 4.0)


def from_root(shard, axis, root):
    mine = lax.axis_index(axis) == root
    return lax.psum(jnp.where(mine, shard, jnp.zeros_like(shard)), axis)


def tile_dist(rows_block, cols_block):
    total = (cols_block[:, 0, :, None] - rows_block[:, 0, None, :]) ** 2
    total = total + (cols_block[:, 1, :, None] - rows_block[:, 1, None, :]) ** 2
    total = total + (cols_block[:, 2, :, None] - rows_block[:, 2, None, :]) ** 2
    return jnp.sqrt(total + 1e-10)


def head_loss(lddt_value, single, ln_gain, w_hidden, b_hidden, w_mid, b_mid, w_logits, b_logits):
    features = single.astype(jnp.float32)
    average = jnp.mean(features, axis=-1, keepdims=True)
    centred = features - average
    variance = jnp.mean(centred * centred, axis=-1, keepdims=True)
    normed = (centred * lax.rsqrt(variance + 1e-05) * ln_gain).astype(jnp.bfloat16)
    first_hidden = jax.nn.relu(
        jnp.dot(normed, w_hidden, preferred_element_type=jnp.float32) + b_hidden
    ).astype(jnp.bfloat16)
    second_hidden = jax.nn.relu(
        jnp.dot(first_hidden, w_mid, preferred_element_type=jnp.float32) + b_mid
    ).astype(jnp.bfloat16)
    logits = jnp.dot(second_hidden, w_logits, preferred_element_type=jnp.float32) + b_logits
    log_total = jnp.log(jnp.sum(jnp.exp(logits), axis=-1))
    bins = logits.shape[-1]
    centers = (jnp.arange(bins).astype(jnp.float32) + 0.5) / bins
    closeness = jnp.exp(-((lddt_value[..., None] - centers) ** 2) * (bins * bins * 0.5))
    target = closeness / jnp.sum(closeness, axis=-1, keepdims=True)
    return log_total - jnp.sum(target * logits, axis=-1)


def local(
    neighbor,
    true_coords,
    pred_coords,
    residue_mask,
    single,
    ln_gain,
    w_hidden,
    b_hidden,
    w_mid,
    b_mid,
    w_logits,
    b_logits,
):
    valid = residue_mask.astype(jnp.float32)
    own_len = residue_mask.shape[1]
    stacked = jnp.concatenate([true_coords, pred_coords, valid[:, None, :]], axis=1)
    row_count = lax.axis_size("row")
    col_count = lax.axis_size("col")
    rows_len = L // row_count
    cols_len = L // col_count
    col_index = lax.axis_index("col")
    rows_part = lax.all_gather(stacked, "col", axis=2, tiled=True)
    offset = col_index * cols_len % rows_len
    column_piece = lax.dynamic_slice_in_dim(rows_part, offset, cols_len, 2)
    source_row = col_index * cols_len // rows_len
    cols_part = from_root(column_piece, "row", source_row)
    true_dist = tile_dist(rows_part[:, 0:3], cols_part[:, 0:3])
    pred_dist = tile_dist(rows_part[:, 3:6], cols_part[:, 3:6])
    mismatch = jnp.abs(pred_dist - true_dist)
    scores = jnp.zeros_like(mismatch)
    for threshold in THRESHOLDS:
        scores = scores + jax.nn.sigmoid(4.0 * (threshold - mismatch))
    scores = 0.25 * scores
    weights = neighbor.astype(jnp.float32) * rows_part[:, 6, None, :] * cols_part[:, 6, :, None]
    preserved = jnp.sum(weights * scores, axis=1)
    neighbors = jnp.sum(weights, axis=1)
    preserved_all, neighbors_all = lax.psum((preserved, neighbors), "col")
    preserved_own = lax.dynamic_slice_in_dim(preserved_all, col_index * own_len, own_len, 1)
    neighbors_own = lax.dynamic_slice_in_dim(neighbors_all, col_index * own_len, own_len, 1)
    lddt_score = preserved_own / jnp.maximum(neighbors_own, 1.0)
    residue_loss = valid * head_loss(
        lddt_score, single, ln_gain, w_hidden, b_hidden, w_mid, b_mid, w_logits, b_logits
    )
    loss_sum, valid_sum = lax.psum((jnp.sum(residue_loss), jnp.sum(valid)), ("row", "col"))
    total_loss = loss_sum / valid_sum
    return (lddt_score, residue_loss, total_loss)


def solution(mesh):
    placed = (
        P(None, "col", "row"),
        P(None, None, ("row", "col")),
        P(None, None, ("row", "col")),
        P(None, ("row", "col")),
        P(None, ("row", "col"), None),
        P(),
        P(),
        P(),
        P(),
        P(),
        P(),
        P(),
    )
    return jax.shard_map(
        local,
        mesh=mesh,
        in_specs=placed,
        out_specs=(P(None, ("row", "col")), P(None, ("row", "col")), P()),
        check_vma=False,
    )
```

profile of v0, /device:TPU:0, one launch (start us, length us, event | category | flops | bytes accessed | tf_op | source)
XLA Modules:
  0.0 312.7 jit_solution(15335422747212448188)
XLA Ops:
  7.3 0.7 convert_bitcast_fusion
  8.0 0.8 pad_maximum_fusion
  8.8 0.9 copy.33
  9.7 21.3 %all_gather.3 = f32[32,7,768]{0,1,2:T(8,128)S(1)} all-gather(f32[32,7,96]{0,1,2:T(8,128)} %copy.33), channel_id=1, replica_groups=mesh['row'=4,'col'=8] {'col'}, dimensions={2}, use_global_device_ids=true | all-gather | bytes 774144 | tf_op jit(solution)/shard_map/all_gather | solution.py:65
  31.0 1.3 dynamic-slice_select_fusion
  32.4 3.3 %fusion.31 = (f32[32,1,768]{0,1,2:T(1,128)}, f32[32,1,768]{0,1,2:T(1,128)}, f32[32,1,768]{0,1,2:T(1,128)}, f32[32,1,768]{0,1,2:T(1,128)}, f32[32,1,768]{0,1,2:T(...) fusion(f32[32,7,768]{0,1,2:T(8,128)S(1)} %all_gather.3), kind=kLoop, calls=%fused_computation.43 | loop fusion | bytes 1376256 | tf_op jit(solution)/shard_map/slice | solution.py:77
  35.6 2.3 convert_reduce_fusion
  37.9 2.8 fusion.4
  40.8 3.2 %maximum_convert_fusion = bf16[32,96,128]{2,1,0:T(8,128)(2,1)S(1)} fusion(bf16[32,96,384]{2,1,0:T(8,128)(2,1)} %param.16, f32[384]{0:T(512)} %param.17, f32[32,96]{1,0:T(8,128)S(1)} %add_rsqrt_fusion, f32[32,96]{1,0:T(8,128)S(1)} %broadcast_multiply_fusion, f32[128]{0:T(128)} %param.21, f32[128]{0:T(128)} %param.19, bf16[384,128]{1,0:T(8,128)(2,1)S(1)} %copy-done, ...), kind=kOutput, calls=%fused_computation.15 | convolution fusion | flops 410910720 | bytes 3303936 | tf_op jit(solution)/shard_map/dot_general | solution.py:32
  44.0 1.1 copy.34
  45.1 1.1 copy.37
  46.2 1.1 copy.39
  47.4 1.1 copy.41
  48.5 1.1 copy.43
  49.7 1.1 copy.45
  50.8 1.1 copy.47
  51.9 1.4 exponential_reduce_fusion
  53.4 48.4 %all-reduce.5.cloned.1.call-done = f32[32,7,384]{0,1,2:T(8,128)} async-done(((f32[32,7,384]{0,1,2:T(8,128)}), f32[32,7,384]{0,1,2:T(8,128)}) %all-reduce.5.cloned.1.call-update) | async-done | bytes 344080 | tf_op jit(solution)/shard_map/psum | solution.py:12
  101.7 6.8 %fusion.32 = (f32[32,1,384]{0,1,2:T(1,128)S(1)}, f32[32,1,384]{0,1,2:T(1,128)S(1)}, f32[32,1,384]{0,1,2:T(1,128)S(1)}, f32[32,1,384]{0,1,2:T(1,128)S(1)}, f32[32...) fusion(f32[32,7,384]{0,1,2:T(8,128)} %all-reduce.5.cloned.1.call-done), kind=kLoop, calls=%fused_computation.44 | loop fusion | bytes 688128 | tf_op jit(solution)/shard_map/slice | solution.py:77
  109.3 98.8 %multiply_reduce_fusion = (f32[32,768]{1,0:T(8,128)}, f32[32,768]{1,0:T(8,128)}) fusion(s32[32,384,768]{2,1,0:T(8,128)} %param.12, f32[32,768]{1,0:T(8,128)S(1)} %copy.47, f32[32,384]{1,0:T(8,128)S(1)} %copy.46, f32[32,768]{1,0:T(8,128)S(1)} %copy.45, f32[32,384]{1,0:T(8,128)S(1)} %copy.44, f32[32,768]{1,0:T(8,128)S(1)} %copy.43, f32[32,384]{1,0:T(8,128)S(1)} %copy.42, ...), kind=kLoop, calls=%fused_computation.1 | loop fusion | flops 471810048 | bytes 38977536 | tf_op jit(solution)/shard_map/reduce_sum | solution.py:78
  208.2 53.1 %all-reduce.7.cloned.1.call-done = (f32[32,768]{1,0:T(8,128)}, f32[32,768]{1,0:T(8,128)}) async-done(((f32[32,768]{1,0:T(8,128)}, f32[32,768]{1,0:T(8,128)}), (f32[32,768]{1,0:T(8,128)}, f32[32,768]{1,0:T(8,128)})) %all-reduce.7.cloned.1.call-update) | async-done | bytes 196624 | tf_op jit(solution)/shard_map/psum | solution.py:80
  261.3 0.9 maximum_divide_fusion
  262.6 1.3 fusion.30
  263.9 39.6 %all-reduce = (f32[]{:T(128)}, f32[]{:T(128)}) all-reduce(f32[]{:T(128)} %get-tuple-element.12, f32[]{:T(128)} %get-tuple-element.28), channel_id=1, replica_groups=mesh['row'=4,'col'=8] {'row','col'}, use_global_device_ids=true, to_apply=%region_11.12 | all-reduce | flops 2 | bytes 16 | tf_op jit(solution)/shard_map/psum | solution.py:87
  (21 shorter events, 1.3 us)
Async XLA Ops:
  7.2 33.6 %copy-start = (bf16[384,128]{1,0:T(8,128)(2,1)S(1)}, bf16[384,128]{1,0:T(8,128)(2,1)}, u32[]{:S(2)}) copy-start(bf16[384,128]{1,0:T(8,128)(2,1)} %param.18) | copy-start | bytes 294916
  7.2 94.6 %all-reduce.5.cloned.1.call-start = ((), (), s32[]{:S(2)}) async-start(), calls=%async_computation | async-start | bytes 3145728 | tf_op jit(solution)/shard_map/psum | solution.py:12
  32.3 228.9 %all-reduce.7.cloned.1.call-start = ((), (), s32[]{:S(2)}) async-start(), calls=%async_computation.1 | async-start | bytes 393216 | tf_op jit(solution)/shard_map/psum | solution.py:80
  109.3 153.3 %copy-start.1 = (s32[32,96]{1,0:T(8,128)S(1)}, s32[32,96]{1,0:T(8,128)}, u32[]{:S(2)}) copy-start(s32[32,96]{1,0:T(8,128)} %param.15) | copy-start | bytes 36868
  262.1 42.6 %copy-start.2 = (f32[32,96]{1,0:T(8,128)}, f32[32,96]{1,0:T(8,128)S(1)}, u32[]{:S(2)}) copy-start(f32[32,96]{1,0:T(8,128)S(1)} %maximum_divide_fusion) | copy-start | bytes 36868
Sparse Core Ops, SparseCore 0:
  32.5 69.2 all-reduce.4
  208.3 52.9 all-reduce.6
where the time goes:
time: 314 us; the launch traced here: 313 us
  other arithmetic  109 us (35%)
  waiting for transfers between devices  102 us (32%)
  blocking collectives  60.8 us (19%)
  local copies, waits for them, and re-layouts  19.7 us (6%)
  between operations  16.6 us (5%)
  matrix products  4.59 us (1%)
    reduce_sum x1, other arithmetic, local(): preserved = jnp.sum(weights * scores, axis=1)  98.8 us
    psum x1, waiting for transfers between devices, local(): preserved_all, neighbors_all = lax.psum((preserved, neighbors), 'col')  53.1 us
    psum x1, waiting for transfers between devices, from_root(): return lax.psum(jnp.where(mine, shard, jnp.zeros_like(shard)), axis)  48.4 us
    psum x1, blocking collectives, local(): lax.psum((jnp.sum(residue_loss), jnp.sum(valid)), ('row', 'col'))  39.6 us
    all_gather x1, blocking collectives, local(): rows_part = lax.all_gather(stacked, 'col', axis=2, tiled=True)  21.3 us
    slice x1, local copies, waits for them, and re-layouts, local(): cols_part[:, 6, :, None]  6.78 us
  transfers between devices with their start and end apart: 2, of which 2 were waited for; matrix products, arithmetic and copies ran while one was open for 7% of the time, Pallas kernels for 0%

commit v1 on v0

--- a/solution.py
+++ b/solution.py
@@ -9,7 +9,7 @@
 
 def from_root(shard, axis, root):
     mine = lax.axis_index(axis) == root
-    return lax.psum(jnp.where(mine, shard, jnp.zeros_like(shard)), axis)
+    return jnp.sum(lax.all_gather(jnp.where(mine, shard, jnp.zeros_like(shard)), axis), axis=0)
 
 
 def tile_dist(rows_block, cols_block):

time: 314 us -> 276 us (0.88)
  waiting for transfers between devices: 102 us -> 66.1 us
  local copies, waits for them, and re-layouts: 19.7 us -> 16 us
    psum x1 -> x0, waiting for transfers between devices: 48.4 us -> none  [from_root(): return lax.psum(jnp.where(mine, shard, jnp.zeros_like(shard)), axis)]
    all_gather x0 -> x1, waiting for transfers between devices: none -> 13 us  [from_root(): lax.all_gather(jnp.where(mine, shard, jnp.zeros_like(shard)), axis)]
    slice x1 -> x0, local copies, waits for them, and re-layouts: 6.78 us -> none  [local(): cols_part[:, 6, :, None]]
  transfers between devices with their start and end apart: 2 -> 2, of which waited for: 2 -> 2; matrix products, arithmetic and copies ran while one was open for 7% -> 8% of each run, Pallas kernels for 0% -> 0%
where the time goes in v1:
time: 276 us; the launch traced here: 275 us
  other arithmetic  111 us (40%)
  waiting for transfers between devices  66.1 us (24%)
  blocking collectives  60.8 us (22%)
  between operations  16.6 us (6%)
  local copies, waits for them, and re-layouts  16 us (6%)
  matrix products  4.6 us (2%)
    reduce_sum x1, other arithmetic, local(): preserved = jnp.sum(weights * scores, axis=1)  98.8 us
    psum x1, waiting for transfers between devices, local(): preserved_all, neighbors_all = lax.psum((preserved, neighbors), 'col')  53 us
    psum x1, blocking collectives, local(): lax.psum((jnp.sum(residue_loss), jnp.sum(valid)), ('row', 'col'))  39.5 us
    all_gather x1, blocking collectives, local(): rows_part = lax.all_gather(stacked, 'col', axis=2, tiled=True)  21.3 us
    all_gather x1, waiting for transfers between devices, from_root(): lax.all_gather(jnp.where(mine, shard, jnp.zeros_like(shard)), axis)  13 us
  transfers between devices with their start and end apart: 2, of which 2 were waited for; matrix products, arithmetic and copies ran while one was open for 8% of the time, Pallas kernels for 0%

profile of v1, /device:TPU:0, one launch (start us, length us, event | category | flops | bytes accessed | tf_op | source)
XLA Modules:
  0.0 275.4 jit_solution(11662590257304280294)
XLA Ops:
  8.8 0.9 copy.38
  9.7 21.3 %all_gather.9 = f32[32,7,768]{0,1,2:T(8,128)S(1)} all-gather(f32[32,7,96]{0,1,2:T(8,128)} %copy.38), channel_id=1, replica_groups=mesh['row'=4,'col'=8] {'col'}, dimensions={2}, use_global_device_ids=true | all-gather | bytes 774144 | tf_op jit(solution)/shard_map/all_gather | solution.py:65
  31.0 1.3 constant_dynamic-slice_fusion
  32.3 2.5 copy.47
  34.8 1.7 broadcast_select_fusion
  36.6 3.3 %fusion.31 = (f32[32,1,768]{0,1,2:T(1,128)}, f32[32,1,768]{0,1,2:T(1,128)}, f32[32,1,768]{0,1,2:T(1,128)}, f32[32,1,768]{0,1,2:T(1,128)}, f32[32,1,768]{0,1,2:T(...) fusion(f32[32,7,768]{0,1,2:T(8,128)S(1)} %all_gather.9), kind=kLoop, calls=%fused_computation.51 | loop fusion | bytes 1376256 | tf_op jit(solution)/shard_map/slice | solution.py:77
  39.9 1.1 copy.39
  41.0 1.1 copy.41
  42.1 1.1 copy.42
  43.3 1.2 copy.43
  44.4 1.1 copy.44
  45.6 1.1 copy.45
  46.7 1.1 copy.46
  47.9 2.3 convert_reduce_fusion
  50.2 2.8 %fusion.4 = f32[32,96]{1,0:T(8,128)S(1)} fusion(bf16[32,96,384]{2,1,0:T(8,128)(2,1)} %param.16, f32[32,96]{1,0:T(8,128)S(1)} %broadcast_multiply_fusion), kind=kLoop, calls=%fused_computation.8 | loop fusion | flops 4715520 | bytes 2383872 | tf_op jit(solution)/shard_map/reduce_sum | solution.py:26
  53.0 3.2 %maximum_convert_fusion = bf16[32,96,128]{2,1,0:T(8,128)(2,1)S(1)} fusion(bf16[32,96,384]{2,1,0:T(8,128)(2,1)} %param.16, f32[384]{0:T(512)} %param.17, f32[32,96]{1,0:T(8,128)S(1)} %add_rsqrt_fusion, f32[32,96]{1,0:T(8,128)S(1)} %broadcast_multiply_fusion, f32[128]{0:T(128)} %param.21, f32[128]{0:T(128)} %param.19, bf16[384,128]{1,0:T(8,128)(2,1)S(1)} %copy-done, ...), kind=kOutput, calls=%fused_computation.15 | convolution fusion | flops 410910720 | bytes 3303936 | tf_op jit(solution)/shard_map/dot_general | solution.py:32
  56.2 1.4 exponential_reduce_fusion
  57.6 13.0 %all-gather.3.cloned.1.call-done = f32[128,7,384]{2,0,1:T(8,128)} async-done(((f32[32,7,384]{2,0,1:T(8,128)}), f32[128,7,384]{2,0,1:T(8,128)}) %all-gather.3.cloned.1.call-update) | async-done | bytes 1376272 | tf_op jit(solution)/shard_map/all_gather | solution.py:12
  70.6 1.5 reduce_sum.90
  72.2 98.8 %multiply_reduce_fusion = (f32[32,768]{1,0:T(8,128)}, f32[32,768]{1,0:T(8,128)}) fusion(s32[32,384,768]{2,1,0:T(8,128)} %param.12, f32[32,768]{1,0:T(8,128)S(1)} %copy.46, f32[32,384]{1,0:T(8,128)S(1)} %get-tuple-element.25, f32[32,768]{1,0:T(8,128)S(1)} %copy.45, f32[32,384]{1,0:T(8,128)S(1)} %get-tuple-element.26, f32[32,768]{1,0:T(8,128)S(1)} %copy.44, ...), kind=kLoop, calls=%fused_computation.1 | loop fusion | flops 471810048 | bytes 38977536 | tf_op jit(solution)/shard_map/reduce_sum | solution.py:78
  171.0 53.0 %all-reduce.4.cloned.1.call-done = (f32[32,768]{1,0:T(8,128)}, f32[32,768]{1,0:T(8,128)}) async-done(((f32[32,768]{1,0:T(8,128)}, f32[32,768]{1,0:T(8,128)}), (f32[32,768]{1,0:T(8,128)}, f32[32,768]{1,0:T(8,128)})) %all-reduce.4.cloned.1.call-update) | async-done | bytes 196624 | tf_op jit(solution)/shard_map/psum | solution.py:80
  224.0 0.9 maximum_divide_fusion
  225.4 1.3 fusion.30
  226.7 39.5 %all-reduce = (f32[]{:T(128)}, f32[]{:T(128)}) all-reduce(f32[]{:T(128)} %get-tuple-element.15, f32[]{:T(128)} %get-tuple-element.31), channel_id=1, replica_groups=mesh['row'=4,'col'=8] {'row','col'}, use_global_device_ids=true, to_apply=%region_11.12 | all-reduce | flops 2 | bytes 16 | tf_op jit(solution)/shard_map/psum | solution.py:87
  (17 shorter events, 2.2 us)
Async XLA Ops:
  7.2 45.8 %copy-start = (bf16[384,128]{1,0:T(8,128)(2,1)S(1)}, bf16[384,128]{1,0:T(8,128)(2,1)}, u32[]{:S(2)}) copy-start(bf16[384,128]{1,0:T(8,128)(2,1)} %param.18) | copy-start | bytes 294916
  7.2 63.5 %all-gather.3.cloned.1.call-start = ((), (), s32[]{:S(2)}) async-start(), calls=%async_computation | async-start | bytes 1720320 | tf_op jit(solution)/shard_map/all_gather | solution.py:12
  36.6 187.5 %all-reduce.4.cloned.1.call-start = ((), (), s32[]{:S(2)}) async-start(), calls=%async_computation.1 | async-start | bytes 393216 | tf_op jit(solution)/shard_map/psum | solution.py:80
  72.1 153.2 %copy-start.1 = (s32[32,96]{1,0:T(8,128)S(1)}, s32[32,96]{1,0:T(8,128)}, u32[]{:S(2)}) copy-start(s32[32,96]{1,0:T(8,128)} %param.15) | copy-start | bytes 36868
  224.9 42.6 %copy-start.2 = (f32[32,96]{1,0:T(8,128)}, f32[32,96]{1,0:T(8,128)S(1)}, u32[]{:S(2)}) copy-start(f32[32,96]{1,0:T(8,128)S(1)} %maximum_divide_fusion) | copy-start | bytes 36868
Sparse Core Ops, SparseCore 0:
  36.7 33.9 all-gather.2
  171.1 52.8 all-reduce.3
